TPU v7x, 32 devices: a whole 2x2x4 slice. The times are simulated.
32 devices in a mesh: mem: 8 (over z, x), blk: 4 (over y, core).
Axes of the slice: x: 2, y: 2, z: 4, core: 2. Of those that a mesh axis runs over, the one named last changes fastest.
Arguments:
- ensemble: bfloat16 [128, 131072], P('mem', 'blk'), may hold values from -6 to 6
- obs_cell: int32 [4, 64, 256], P('blk', 'mem'), may hold values from 0 to 511
- obs_count: int32 [4, 64], P('blk', 'mem'), may hold values from 1 to 256, 10240 in all within a row
- obs_value: float32 [4, 64, 256], P('blk', 'mem'), may hold values from -6 to 6
- obs_rinv: float32 [4, 64, 256], P('blk', 'mem'), may hold values from 0.05 to 0.5
Outputs:
- increments: bfloat16 [128, 131072], P('mem', 'blk')
Inputs may be any that keep to these rules, and one draw needn't show every extreme that they name: `obs_cell`: slots at or past the block's count are unused. `obs_count`: the counts of one band sum to 10240, and some block holds exactly 256.
All inputs are finite; a program needn't handle non-finite values. Where the computation divides by a largest or mean magnitude, that divisor is 1e-20 or more.
Results may differ from a plain program's by a relative error of at most 0.0051.
Values may be sent and summed in bfloat16 or wider, within the bound.
A program may use at most 64 MiB of HBM per device.

v0:
```python
import jax
import jax.numpy as jnp
from jax import lax
from jax.sharding import PartitionSpec as P

NS_ITERS = 4


localize = 0.5
inflation = 1.1


def with_halo(block, sides, width):
    for axis, dim in sides:
        count = lax.axis_size(axis)
        forward = [(i, i + 1) for i in range(count - 1)]
        forward.append((count - 1, 0))
        backward = [(target, source) for source, target in forward]
        low = lax.ppermute(
            lax.slice_in_dim(block, block.shape[dim] - width, None, axis=dim), axis, forward
        )
        high = lax.ppermute(lax.slice_in_dim(block, 0, width, axis=dim), axis, backward)
        block = jnp.concatenate([low, block, high], axis=dim)
    return block


def center_blocks(members):
    values = jnp.transpose(members.astype(jnp.float32), (1, 0, 2))
    average = jnp.mean(values, axis=1)
    return (values - average[:, None, :], average)


def observe(deviation, average, cell_ids, live_counts, obs_values, inv_var):
    cell_width = deviation.shape[2]
    positions = lax.broadcasted_iota(jnp.int32, cell_ids.shape + (cell_width,), 2)
    selector = (positions == cell_ids[:, :, None]).astype(jnp.float32)
    sampled = jnp.einsum("bkc,boc->bko", deviation, selector, precision=lax.Precision.HIGHEST)
    obs_mean = jnp.einsum("bc,boc->bo", average, selector, precision=lax.Precision.HIGHEST)
    slots = lax.broadcasted_iota(jnp.int32, cell_ids.shape, 1)
    live = (slots < live_counts[:, None]).astype(jnp.float32)
    weight_root = live * jnp.sqrt(inv_var)
    upper = sampled * weight_root[:, None, :]
    lower = (weight_root * (obs_values - obs_mean))[:, None, :]
    return jnp.concatenate([upper, lower], axis=1).astype(jnp.bfloat16)


def gram_of(obs_rows):
    return jnp.einsum("bko,bjo->bkj", obs_rows, obs_rows, preferred_element_type=jnp.float32)


def batch_mm(left, right):
    return jnp.einsum("bij,bjk->bik", left, right, precision=lax.Precision.HIGHEST)


def transform_apply(localized, deviation):
    ensemble_size = deviation.shape[1]
    identity = jnp.eye(ensemble_size, dtype=jnp.float32)
    system = (ensemble_size - 1) / inflation * identity + localized[
        :, :ensemble_size, :ensemble_size
    ]
    forcing = localized[:, :ensemble_size, ensemble_size]
    bound_norm = jnp.max(jnp.sum(jnp.abs(system), axis=2), axis=1)
    approx_y = system / bound_norm[:, None, None]
    approx_z = jnp.broadcast_to(identity, system.shape)
    for iteration in range(NS_ITERS):
        update = 1.5 * identity - 0.5 * batch_mm(approx_z, approx_y)
        approx_y = batch_mm(approx_y, update)
        approx_z = batch_mm(update, approx_z)
    root_inv = approx_z / jnp.sqrt(bound_norm)[:, None, None]
    inner = jnp.einsum("bij,bj->bi", root_inv, forcing, precision=lax.Precision.HIGHEST)
    mean_weights = jnp.einsum("bij,bj->bi", root_inv, inner, precision=lax.Precision.HIGHEST)
    mixing = (
        jnp.sqrt(jnp.float32(ensemble_size - 1)) * root_inv + mean_weights[:, :, None] - identity
    )
    increment = jnp.einsum("bjc,bjk->kbc", deviation, mixing, precision=lax.Precision.HIGHEST)
    return increment.astype(jnp.bfloat16)


def on_device(ensemble, obs_cell, obs_count, obs_value, obs_rinv):
    groups = lax.axis_size("mem")
    local_members = ensemble.shape[0]
    blocks = obs_cell.shape[1]
    cell_width = ensemble.shape[1] // (groups * blocks)
    pieces = ensemble.reshape(local_members, groups, blocks, cell_width)
    arrived = lax.all_to_all(pieces, "mem", split_axis=1, concat_axis=0, tiled=True)
    deviation, average = center_blocks(arrived[:, 0])
    obs_rows = observe(deviation, average, obs_cell[0], obs_count[0], obs_value[0], obs_rinv[0])
    padded_rows = with_halo(obs_rows, (("mem", 0),), 1)
    padded = gram_of(padded_rows)
    localized = padded[1:-1] + localize * (padded[:-2] + padded[2:])
    increment = transform_apply(localized, deviation)
    ensemble_size = increment.shape[0]
    outgoing = increment.reshape(ensemble_size, 1, blocks * cell_width)
    returned = lax.all_to_all(outgoing, "mem", split_axis=0, concat_axis=1, tiled=True)
    return returned.reshape(local_members, groups * blocks * cell_width)


def solution(mesh):
    placed = (
        P("mem", "blk"),
        P("blk", "mem", None),
        P("blk", "mem"),
        P("blk", "mem", None),
        P("blk", "mem", None),
    )
    return jax.shard_map(
        on_device, mesh=mesh, in_specs=placed, out_specs=P("mem", "blk"), check_vma=False
    )
```

profile of v0, /device:TPU:0, one launch (start us, length us, event | category | flops | bytes accessed | tf_op | source)
XLA Modules:
  0.0 100.4 jit_solution(12900791713028595569)
XLA Ops:
  0.0 1.5 %copy.73 = bf16[2,8,64,512]{3,2,1,0:T(8,128)(2,1)S(1)} copy(bf16[2,8,64,512]{3,1,2,0:T(8,128)(2,1)} %bitcast.94) | data formatting | bytes 2097152
  1.5 1.1 %copy.54 = bf16[16,8,8,512]{3,2,0,1:T(8,128)(2,1)} copy(bf16[16,8,8,512]{3,2,1,0:T(8,128)(2,1)S(1)} %bitcast.93) | data formatting | bytes 2097152 | tf_op jit(solution)/shard_map/reshape | solution.py:84
  2.6 7.3 %all-to-all-start = ((bf16[16,8,8,512]{3,2,0,1:T(8,128)(2,1)}), bf16[16,8,8,512]{3,2,0,1:T(8,128)(2,1)S(1)}, u32[]{:S(2)}, u32[]{:S(2)}) async-start(bf16[16,8,8,512]{3,2,0,1:T(8,128)(2,1)} %copy.54), calls=%async_computation | async-start | bytes 2097152 | tf_op jit(solution)/shard_map/all_to_all | solution.py:85
  10.1 25.5 %all-to-all-done = bf16[16,8,8,512]{3,2,0,1:T(8,128)(2,1)S(1)} async-done(((bf16[16,8,8,512]{3,2,0,1:T(8,128)(2,1)}), bf16[16,8,8,512]{3,2,0,1:T(8,128)(2,1)S(1)}, u32[]{:S(2)}, u32[]{:S(2)}) %all-to-all-start) | async-done | bytes 1048608 | tf_op jit(solution)/shard_map/all_to_all | solution.py:85
  36.0 1.1 %bitcast_reduce_fusion = f32[8,512]{1,0:T(8,128)S(1)} fusion(f32[128,8,512]{2,1,0:T(8,128)S(1)} %bitcast.88), kind=kLoop, calls=%fused_computation.4 | loop fusion | flops 520192 | bytes 2113536 | tf_op jit(solution)/shard_map/reduce_sum | solution.py:29
  37.1 2.2 %fusion = f32[8,1,256]{2,1,0:T(1,128)S(1)} fusion(s32[8,256]{1,0:T(8,128)S(1)} %bitcast.97, f32[8,512,1]{1,0,2:T(8,128)S(1)} %get-tuple-element.9), kind=kOutput, calls=%fused_computation.1 | convolution fusion | flops 13631488 | bytes 32768 | tf_op jit(solution)/shard_map/bc,boc->bo/dot_general | solution.py:38
  39.4 3.5 %fusion.10 = bf16[8,128,256]{2,1,0:T(8,128)(2,1)S(1)} fusion(s32[8,256]{1,0:T(8,128)S(1)} %bitcast.98, f32[128,8,512]{2,1,0:T(8,128)S(1)} %bitcast.89, f32[8,512]{1,0:T(8,128)S(1)} %get-tuple-element.10, f32[8,256]{1,0:T(8,128)S(1)} %get-tuple-element.6), kind=kOutput, calls=%fused_computation.13 | convolution fusion | flops 1612709888 | bytes 2654208 | tf_op jit(solution)/shard_map/bkc,boc->bko/dot_general | solution.py:37
  42.9 1.5 %collective-permute-start = (bf16[1,129,256]{2,1,0:T(8,128)(2,1)S(1)}, bf16[1,129,256]{2,1,0:T(8,128)(2,1)S(1)}, u32[]{:S(2)}, u32[]{:S(2)}) collective-permute-start(bf16[1,129,256]{2,1,0:T(8,128)(2,1)S(1)} %get-tuple-element.7), channel_id=1, source_target_pairs={{0,4},{4,8},{8,12},{12,16},{16,20},{20,24},{24,28},{28,0},{1,5},{5... | collective-permute-start | bytes 198152 | tf_op jit(solution)/shard_map/ppermute | solution.py:19
  44.4 3.3 %collective-permute-start.1 = (bf16[1,129,256]{2,1,0:T(8,128)(2,1)S(1)}, bf16[1,129,256]{2,1,0:T(8,128)(2,1)S(1)}, u32[]{:S(2)}, u32[]{:S(2)}) collective-permute-start(bf16[1,129,256]{2,1,0:T(8,128)(2,1)S(1)} %get-tuple-element.8), channel_id=1, source_target_pairs={{4,0},{8,4},{12,8},{16,12},{20,16},{24,20},{28,24},{0,28},{5,1},{9... | collective-permute-start | bytes 198152 | tf_op jit(solution)/shard_map/ppermute | solution.py:22
  47.7 2.3 %collective-permute-done = bf16[1,129,256]{2,1,0:T(8,128)(2,1)S(1)} collective-permute-done((bf16[1,129,256]{2,1,0:T(8,128)(2,1)S(1)}, bf16[1,129,256]{2,1,0:T(8,128)(2,1)S(1)}, u32[]{:S(2)}, u32[]{:S(2)}) %collective-permute-start) | collective-permute-done | bytes 66080 | tf_op jit(solution)/shard_map/ppermute | solution.py:19
  50.7 1.3 %fusion.14 = f32[8,128,128]{2,1,0:T(8,128)S(1)} fusion(f32[128,128]{1,0:T(8,128)S(1)} %copy.53, f32[128,128]{1,0:T(8,128)S(1)} %copy.52, f32[8,129,129]{1,2,0:T(8,128)S(1)} %fusion.16, f32[8]{0:T(128)S(1)} %reduce_max.9, f32[128,128]{0,1:T(8,128)S(1)} %fusion.37), kind=kOutput, calls=%fused_computation.22 | convolution fusion | flops 201850880 | bytes 1245696 | tf_op jit(solution)/shard_map/bij,bjk->bik/dot_general | solution.py:52
  52.0 1.1 %fusion.48 = f32[8,128,128]{2,1,0:T(8,128)S(1)} fusion(f32[8,128,128]{2,1,0:T(8,128)S(1)} %fusion.14, f32[8,129,129]{1,2,0:T(8,128)S(1)} %fusion.16, f32[8]{0:T(128)S(1)} %reduce_max.9, f32[128,128]{0,1:T(8,128)S(1)} %fusion.37), kind=kOutput, calls=%fused_computation.68 | convolution fusion | flops 201588736 | bytes 1638912 | tf_op jit(solution)/shard_map/bij,bjk->bik/dot_general | solution.py:52
  53.1 0.6 fusion.34
  53.6 0.6 fusion.13
  54.3 0.6 fusion.52
  55.0 0.6 fusion.51
  55.6 0.6 fusion.12
  56.3 0.6 fusion.54
  56.9 0.6 fusion.53
  57.6 0.6 fusion.11
  58.2 0.6 convolution_divide_fusion
  58.9 0.9 convolution_bitcast_fusion
  59.8 0.9 fusion.55
  60.7 3.4 %fusion.8 = bf16[128,8,512]{2,0,1:T(8,128)(2,1)S(1)} fusion(f32[128,8,512]{2,1,0:T(8,128)S(1)} %bitcast.90, f32[8,512]{1,0:T(8,128)S(1)} %get-tuple-element.10, f32[8,128,128]{2,1,0:T(8,128)S(1)} %convolution_divide_fusion, f32[8,128]{1,0:T(8,128)S(1)} %bitcast.95, f32[128,128]{1,0:T(8,128)S(1)} %copy.53), kind=kOutput, calls=%fused_computation.11 | convolution fusion | flops 806748160 | bytes 3756032 | tf_op jit(solution)/shard_map/bjc,bjk->kbc/dot_general | solution.py:75
  64.2 0.7 copy.60
  65.3 1.4 %reduce = bf16[128,4096]{0,1:T(8,128)(2,1)S(1)} reduce(bf16[128,1,4096]{0,2,1:T(8,128)(2,1)S(1)} %bitcast.92, bf16[]{:T(256)} %broadcast.59), dimensions={1}, to_apply=%copy.61.reduce_sub_computation | reduce | bytes 2097154 | tf_op jit(solution)/shard_map/reshape | solution.py:93
  66.8 0.5 copy.98
  67.3 0.8 reshape.78
  68.1 29.0 %all_to_all.24 = bf16[8,2,32768]{2,1,0:T(2,128)(2,1)S(1)} all-to-all(bf16[8,2,32768]{2,1,0:T(2,128)(2,1)S(1)} %reshape.78), channel_id=1, replica_groups=mesh['mem'=8,'blk'=4] {'mem'}, dimensions={0} | all-to-all | bytes 2097152 | tf_op jit(solution)/shard_map/all_to_all | solution.py:94
  97.2 1.0 %reshape.79 = bf16[128,1,4096]{2,1,0:T(2,128)(2,1)S(1)} reshape(bf16[8,2,32768]{2,1,0:T(2,128)(2,1)S(1)} %all_to_all.24) | data formatting | bytes 2097152
  98.2 1.1 %copy.72 = bf16[128,1,4096]{2,0,1:T(8,128)(2,1)S(1)} copy(bf16[128,1,4096]{2,1,0:T(2,128)(2,1)S(1)} %reshape.79) | data formatting | bytes 2097152
  99.4 1.0 %copy.74 = bf16[2,8,8,4096]{3,1,2,0:T(8,128)(2,1)} copy(bf16[2,8,8,4096]{3,1,0,2:T(8,128)(2,1)S(1)} %bitcast.91) | data formatting | bytes 2097152
  (25 shorter events, 1.8 us)
Async XLA Ops:
  2.6 33.0 %all-to-all-start = ((bf16[16,8,8,512]{3,2,0,1:T(8,128)(2,1)}), bf16[16,8,8,512]{3,2,0,1:T(8,128)(2,1)S(1)}, u32[]{:S(2)}, u32[]{:S(2)}) async-start(bf16[16,8,8,512]{3,2,0,1:T(8,128)(2,1)} %copy.54), calls=%async_computation | async-start | bytes 2097152 | tf_op jit(solution)/shard_map/all_to_all | solution.py:85
  35.9 1.2 %copy-start.3 = (s32[1,8,256]{2,1,0:T(8,128)S(1)}, s32[1,8,256]{2,1,0:T(8,128)}, u32[]{:S(2)}) copy-start(s32[1,8,256]{2,1,0:T(8,128)} %param.6) | copy-start | bytes 24580
  36.0 3.4 %copy-start = (f32[1,8,256]{2,1,0:T(8,128)S(1)}, f32[1,8,256]{2,1,0:T(8,128)}, u32[]{:S(2)}) copy-start(f32[1,8,256]{2,1,0:T(8,128)} %param.8) | copy-start | bytes 24580
  36.0 3.4 %copy-start.1 = (f32[1,8,256]{2,1,0:T(8,128)S(1)}, f32[1,8,256]{2,1,0:T(8,128)}, u32[]{:S(2)}) copy-start(f32[1,8,256]{2,1,0:T(8,128)} %param.9) | copy-start | bytes 24580
  36.0 3.4 %copy-start.2 = (s32[1,8]{1,0:T(1,128)S(1)}, s32[1,8]{1,0:T(1,128)}, u32[]{:S(2)}) copy-start(s32[1,8]{1,0:T(1,128)} %param.7) | copy-start | bytes 100
  42.9 7.1 %collective-permute-start = (bf16[1,129,256]{2,1,0:T(8,128)(2,1)S(1)}, bf16[1,129,256]{2,1,0:T(8,128)(2,1)S(1)}, u32[]{:S(2)}, u32[]{:S(2)}) collective-permute-start(bf16[1,129,256]{2,1,0:T(8,128)(2,1)S(1)} %get-tuple-element.7), channel_id=1, source_target_pairs={{0,4},{4,8},{8,12},{12,16},{16,20},{20,24},{24,28},{28,0},{1,5},{5... | collective-permute-start | bytes 198152 | tf_op jit(solution)/shard_map/ppermute | solution.py:19
  44.4 5.6 %collective-permute-start.1 = (bf16[1,129,256]{2,1,0:T(8,128)(2,1)S(1)}, bf16[1,129,256]{2,1,0:T(8,128)(2,1)S(1)}, u32[]{:S(2)}, u32[]{:S(2)}) collective-permute-start(bf16[1,129,256]{2,1,0:T(8,128)(2,1)S(1)} %get-tuple-element.8), channel_id=1, source_target_pairs={{4,0},{8,4},{12,8},{16,12},{20,16},{24,20},{28,24},{0,28},{5,1},{9... | collective-permute-start | bytes 198152 | tf_op jit(solution)/shard_map/ppermute | solution.py:22
where the time goes:
time: 101 us; the launch traced here: 100 us
  blocking collectives  29 us (29%)
  waiting for transfers between devices  27.8 us (28%)
  matrix products  19.4 us (19%)
  starting transfers between devices  12.1 us (12%)
  local copies, waits for them, and re-layouts  8.56 us (8%)
  other arithmetic  3.24 us (3%)
    all_to_all x1, blocking collectives, on_device(): lax.all_to_all(outgoing, 'mem', split_axis=0, concat_axis=1, tiled=True)  29 us
    all_to_all x1, waiting for transfers between devices, on_device(): lax.all_to_all(pieces, 'mem', split_axis=1, concat_axis=0, tiled=True)  25.5 us
    dot_general x11, matrix products, batch_mm(): jnp.einsum('bij,bjk->bik', left, right, precision=lax.Precision.HIGHEST)  8.15 us
    all_to_all x1, starting transfers between devices, on_device(): lax.all_to_all(pieces, 'mem', split_axis=1, concat_axis=0, tiled=True)  7.28 us
    unnamed x14, local copies, waits for them, and re-layouts  6.12 us
    dot_general x1, matrix products, observe(): jnp.einsum('bkc,boc->bko', deviation, selector, precision=lax.Precision.H...  3.46 us
    dot_general x1, matrix products, transform_apply(): jnp.einsum('bjc,bjk->kbc', deviation, mixing, precision=lax.Precision.HIG...  3.4 us
    ppermute x1, starting transfers between devices, with_halo(): lax.ppermute(lax.slice_in_dim(block, 0, width, axis=dim), axis, backward)  3.3 us
  transfers between devices with their start and end apart: 3, of which 2 were waited for; matrix products, arithmetic and copies ran while one was open for 0% of the time, Pallas kernels for 0%

commit v1 on v0

--- a/solution.py
+++ b/solution.py
@@ -1,6 +1,10 @@
+import functools
+
 import jax
 import jax.numpy as jnp
 from jax import lax
+from jax.experimental import pallas as pl
+from jax.experimental.pallas import tpu as pltpu
 from jax.sharding import PartitionSpec as P
 
 NS_ITERS = 4
@@ -8,6 +12,251 @@
 
 localize = 0.5
 inflation = 1.1
+
+MESH = pl.DeviceIdType.MESH
+F32 = jnp.float32
+BF16 = jnp.bfloat16
+
+
+def halves(x):
+    high = x.astype(BF16)
+    return high, (x - high.astype(F32)).astype(BF16)
+
+
+def as_left(x):
+    return jnp.concatenate(halves(x), axis=1)
+
+
+def as_right(x):
+    wide = jnp.concatenate(halves(x), axis=1)
+    return jnp.concatenate([wide, wide], axis=0)
+
+
+def mm(left, right):
+    both = jnp.dot(left, right, preferred_element_type=F32)
+    size = both.shape[1] // 2
+    return both[:, :size] + both[:, size:]
+
+
+def observed_rows(members, selector, values, root):
+    ensemble_size = members.shape[0]
+    sampled = jnp.dot(members, selector, preferred_element_type=F32)
+    obs_mean = jnp.sum(sampled, axis=0, keepdims=True) * (1.0 / ensemble_size)
+    upper = ((sampled - obs_mean) * root).astype(BF16)
+    lower = root * (values - obs_mean)
+    place = lax.broadcasted_iota(jnp.int32, (16, lower.shape[1]), 0)
+    lower = jnp.where(place == 0, jnp.broadcast_to(lower, place.shape), 0.0).astype(BF16)
+    return jnp.concatenate([upper, lower], axis=0)
+
+
+def increments_of(localized, members):
+    ensemble_size = members.shape[0]
+    row = lax.broadcasted_iota(jnp.int32, (ensemble_size, ensemble_size), 0)
+    column = lax.broadcasted_iota(jnp.int32, (ensemble_size, ensemble_size), 1)
+    identity = (row == column).astype(F32)
+    system = (ensemble_size - 1) / inflation * identity + localized[:ensemble_size]
+    bound_norm = jnp.max(
+        jnp.sum(jnp.abs(system), axis=0, keepdims=True), axis=1, keepdims=True
+    )
+    approx_y = system / bound_norm
+    update = 1.5 * identity - 0.5 * approx_y
+    approx_z = update
+    for iteration in range(1, NS_ITERS):
+        approx_y = mm(as_left(approx_y), as_right(update))
+        left_z = as_left(approx_z)
+        update = 1.5 * identity - 0.5 * mm(left_z, as_right(approx_y))
+        approx_z = mm(left_z, as_right(update))
+    root_inv = approx_z / jnp.sqrt(bound_norm)
+    right_r = as_right(root_inv)
+    inner = mm(as_left(localized[ensemble_size:]), right_r)
+    mean_weights = mm(as_left(inner), right_r)[0:1]
+    mixing = jnp.sqrt(F32(ensemble_size - 1)) * root_inv + mean_weights - identity
+    high, low = halves(mixing)
+    row_sum = jnp.sum(high.astype(F32) + low.astype(F32), axis=1, keepdims=True)
+    average = jnp.sum(members.astype(F32), axis=0, keepdims=True) * (1.0 / ensemble_size)
+    total = jnp.dot(
+        jnp.concatenate([high, low], axis=1),
+        jnp.concatenate([members, members], axis=0),
+        preferred_element_type=F32,
+    )
+    return (total - row_sum * average).astype(BF16)
+
+
+def kernel(
+    groups,
+    ens,
+    cell,
+    count,
+    value,
+    rinv,
+    out,
+    arrived,
+    rows,
+    gram,
+    selector,
+    stage,
+    weight,
+    own_sem,
+    fwd_send,
+    fwd_recv,
+    ret_send,
+    ret_recv,
+    halo_send,
+    halo_recv,
+):
+    me = lax.axis_index("mem")
+    blocks, _, width = arrived.shape
+    local = ens.shape[0]
+    slots = cell.shape[1]
+    size = groups * local
+
+    barrier = pltpu.get_barrier_semaphore()
+    for step in range(1, groups):
+        pl.semaphore_signal(
+            barrier, inc=1, device_id={"mem": lax.rem(me + step, groups)}, device_id_type=MESH
+        )
+
+    weight[...] = jnp.sqrt(rinv[...])
+
+    @pl.loop(0, blocks)
+    def _(b):
+        positions = lax.broadcasted_iota(jnp.int32, (width, slots), 0)
+        selector[b] = jnp.where(positions == cell[pl.ds(b, 1), :], 1.0, 0.0).astype(BF16)
+
+    pl.semaphore_wait(barrier, groups - 1)
+
+    def columns(owner, b):
+        start = pl.multiple_of((owner * blocks + b) * width, width)
+        return pl.ds(start, width)
+
+    def members_of(owner):
+        return pl.ds(pl.multiple_of(owner * local, local), local)
+
+    @pl.loop(0, blocks)
+    def _(i):
+        b = lax.rem(i + blocks - 1, blocks)
+        for step in range(1, groups):
+            peer = lax.rem(me + step, groups)
+            pltpu.make_async_remote_copy(
+                src_ref=ens.at[:, columns(peer, b)],
+                dst_ref=arrived.at[b, members_of(me), :],
+                send_sem=fwd_send,
+                recv_sem=fwd_recv.at[b],
+                device_id={"mem": peer},
+                device_id_type=MESH,
+            ).start()
+        pltpu.make_async_copy(
+            ens.at[:, columns(me, b)], arrived.at[b, members_of(me), :], fwd_recv.at[b]
+        ).start()
+
+    def form_gram(slot):
+        held = rows[slot]
+        gram[slot] = lax.dot_general(
+            held, held[:size], (((1,), (1,)), ((), ())), preferred_element_type=F32
+        )
+
+    def take_block(b):
+        pltpu.make_async_copy(arrived.at[b], arrived.at[b], fwd_recv.at[b]).wait()
+        alive = lax.broadcasted_iota(jnp.int32, (1, slots), 1) < count[0, b]
+        root = jnp.where(alive, weight[pl.ds(b, 1), :], 0.0)
+        rows[b + 1] = observed_rows(arrived[b], selector[b], value[pl.ds(b, 1), :], root)
+
+    def give_block(b):
+        localized = gram[b + 1] + localize * (gram[b] + gram[b + 2])
+        stage[b] = increments_of(localized, arrived[b])
+        for step in range(1, groups):
+            peer = lax.rem(me + step, groups)
+            pltpu.make_async_remote_copy(
+                src_ref=stage.at[b, members_of(peer), :],
+                dst_ref=out.at[:, columns(me, b)],
+                send_sem=ret_send,
+                recv_sem=ret_recv,
+                device_id={"mem": peer},
+                device_id_type=MESH,
+            ).start()
+        pltpu.make_async_copy(
+            stage.at[b, members_of(me), :], out.at[:, columns(me, b)], own_sem
+        ).start()
+
+    def halo(source, target, peer, which):
+        return pltpu.make_async_remote_copy(
+            src_ref=rows.at[source],
+            dst_ref=rows.at[target],
+            send_sem=halo_send.at[which],
+            recv_sem=halo_recv.at[which],
+            device_id={"mem": peer},
+            device_id_type=MESH,
+        )
+
+    upward = halo(blocks, 0, lax.rem(me + 1, groups), 0)
+    downward = halo(1, blocks + 1, lax.rem(me + groups - 1, groups), 1)
+
+    take_block(blocks - 1)
+    upward.start()
+    form_gram(blocks)
+    take_block(0)
+    downward.start()
+    form_gram(1)
+    take_block(1)
+    form_gram(2)
+    upward.wait_recv()
+    form_gram(0)
+    give_block(0)
+
+    @pl.loop(2, blocks - 1)
+    def _(b):
+        take_block(b)
+        form_gram(b + 1)
+        give_block(b - 1)
+
+    downward.wait_recv()
+    form_gram(blocks + 1)
+
+    @pl.loop(blocks - 2, blocks)
+    def _(b):
+        give_block(b)
+
+    upward.wait_send()
+    downward.wait_send()
+    share = blocks * width
+    afar = pl.ds(0, (groups - 1) * share)
+    pltpu.make_async_copy(ens.at[:, afar], ens.at[:, afar], fwd_send).wait()
+    pltpu.make_async_copy(out.at[:, afar], out.at[:, afar], ret_send).wait()
+    pltpu.make_async_copy(out.at[:, afar], out.at[:, afar], ret_recv).wait()
+    near = pl.ds(0, share)
+    pltpu.make_async_copy(out.at[:, near], out.at[:, near], own_sem).wait()
+
+
+def fused(ensemble, obs_cell, obs_count, obs_value, obs_rinv):
+    groups = lax.axis_size("mem")
+    local, cells = ensemble.shape
+    blocks, slots = obs_cell.shape[1:]
+    width = cells // (groups * blocks)
+    size = groups * local
+    whole = pl.BlockSpec(memory_space=pltpu.VMEM)
+    return pl.pallas_call(
+        functools.partial(kernel, groups),
+        out_shape=jax.ShapeDtypeStruct(ensemble.shape, BF16),
+        in_specs=[whole, whole, pl.BlockSpec(memory_space=pltpu.SMEM), whole, whole],
+        out_specs=whole,
+        scratch_shapes=[
+            pltpu.VMEM((blocks, size, width), BF16),
+            pltpu.VMEM((blocks + 2, size + 16, slots), BF16),
+            pltpu.VMEM((blocks + 2, size + 16, size), F32),
+            pltpu.VMEM((blocks, width, slots), BF16),
+            pltpu.VMEM((blocks, size, width), BF16),
+            pltpu.VMEM((blocks, slots), F32),
+            pltpu.SemaphoreType.DMA,
+            pltpu.SemaphoreType.DMA,
+            pltpu.SemaphoreType.DMA((blocks,)),
+            pltpu.SemaphoreType.DMA,
+            pltpu.SemaphoreType.DMA,
+            pltpu.SemaphoreType.DMA((2,)),
+            pltpu.SemaphoreType.DMA((2,)),
+        ],
+        compiler_params=pltpu.CompilerParams(collective_id=0, has_side_effects=True),
+        name="letkf",
+    )(ensemble, obs_cell[0], obs_count, obs_value[0], obs_rinv[0])
 
 
 def with_halo(block, sides, width):
@@ -95,6 +344,16 @@
     return returned.reshape(local_members, groups * blocks * cell_width)
 
 
+def by_shape(ensemble, *observations):
+    groups = lax.axis_size("mem")
+    local, cells = ensemble.shape
+    blocks, slots = observations[0].shape[1:]
+    width = cells // (groups * blocks)
+    aligned = local % 16 == 0 and width % 128 == 0 and slots % 128 == 0
+    aligned = aligned and (groups * local) % 128 == 0 and groups > 1 and blocks > 2
+    return (fused if aligned else on_device)(ensemble, *observations)
+
+
 def solution(mesh):
     placed = (
         P("mem", "blk"),
@@ -104,5 +363,5 @@
         P("blk", "mem", None),
     )
     return jax.shard_map(
-        on_device, mesh=mesh, in_specs=placed, out_specs=P("mem", "blk"), check_vma=False
-    )
+        by_shape, mesh=mesh, in_specs=placed, out_specs=P("mem", "blk"), check_vma=False
+    )

time: 101 us -> 62.4 us (0.62)
  Pallas kernels: 0 us -> 59.9 us
  blocking collectives: 29 us -> 0 us
  waiting for transfers between devices: 27.8 us -> 0 us
  matrix products: 19.4 us -> 0 us
  starting transfers between devices: 12.1 us -> 0 us
  local copies, waits for them, and re-layouts: 8.56 us -> 2.26 us
  other arithmetic: 3.24 us -> 0 us
    pallas_call x0 -> x1, Pallas kernels: none -> 59.9 us  [fused(): pl.pallas_call(functools.partial(kernel, groups), out_shape=jax.ShapeDtyp...]
    all_to_all x1 -> x0, blocking collectives: 29 us -> none  [on_device(): lax.all_to_all(outgoing, 'mem', split_axis=0, concat_axis=1, tiled=True)]
    all_to_all x1 -> x0, waiting for transfers between devices: 25.5 us -> none  [on_device(): lax.all_to_all(pieces, 'mem', split_axis=1, concat_axis=0, tiled=True)]
    dot_general x17 -> x0, matrix products: 19.4 us -> none  [the longest x11 8.15 us: batch_mm(): jnp.einsum('bij,bjk->bik', left, right, precision=lax.Precision.HIGHEST)]
    all_to_all x1 -> x0, starting transfers between devices: 7.28 us -> none  [on_device(): lax.all_to_all(pieces, 'mem', split_axis=1, concat_axis=0, tiled=True)]
    ppermute x2 -> x0, starting transfers between devices: 4.78 us -> none  [the longest x1 3.3 us: with_halo(): lax.ppermute(lax.slice_in_dim(block, 0, width, axis=dim), axis, backward)]
    unnamed x14 -> x1, local copies, waits for them, and re-layouts: 6.12 us -> 2.26 us
    ppermute x2 -> x0, waiting for transfers between devices: 2.27 us -> none  [the longest x1 2.27 us: with_halo(): lax.ppermute(lax.slice_in_dim(block, block.shape[dim] - width, None, axis...]
  transfers between devices with their start and end apart: 3 -> 0, of which waited for: 2 -> 0; matrix products, arithmetic and copies ran while one was open for 0% -> 0% of each run, Pallas kernels for 0% -> 0%
where the time goes in v1:
time: 62.4 us; the launch traced here: 62.2 us
  Pallas kernels  59.9 us (96%)
  local copies, waits for them, and re-layouts  2.26 us (4%)
    pallas_call x1, Pallas kernels, fused(): pl.pallas_call(functools.partial(kernel, groups), out_shape=jax.ShapeDtyp...  59.9 us
    unnamed x1, local copies, waits for them, and re-layouts  2.26 us

profile of v1, /device:TPU:0, one launch (start us, length us, event | category | flops | bytes accessed | tf_op | source)
XLA Modules:
  0.0 62.2 jit_solution(518982574034655413)
XLA Ops:
  0.0 59.9 %letkf.1 = bf16[16,32768]{1,0:T(8,128)(2,1)} custom-call(bf16[16,32768]{1,0:T(8,128)(2,1)} %ens.1, s32[8,256]{1,0:T(8,128)} %bitcast.3, s32[1,8]{1,0:T(1,128)} %count.1, f32[8,256]{1,0:T(8,128)} %bitcast.4, f32[8,256]{1,0:T(8,128)} %bitcast.5), custom_call_target="tpu_custom_call" | custom-call | tf_op jit(solution)/shard_map/letkf/pallas_call | solution.py:237
  59.9 2.3 %copy.7 = bf16[16,32768]{1,0:T(8,128)(2,1)} copy(bf16[16,32768]{1,0:T(8,128)(2,1)} %letkf.1) | data formatting | bytes 2097152

commit v2 on v1

--- a/solution.py
+++ b/solution.py
@@ -14,6 +14,7 @@
 inflation = 1.1
 
 MESH = pl.DeviceIdType.MESH
+WINDOW = 3
 F32 = jnp.float32
 BF16 = jnp.bfloat16
 
@@ -84,7 +85,7 @@
 
 def kernel(
     groups,
-    ens,
+    ens_hbm,
     cell,
     count,
     value,
@@ -96,6 +97,8 @@
     selector,
     stage,
     weight,
+    ens,
+    load_sem,
     own_sem,
     fwd_send,
     fwd_recv,
@@ -110,6 +113,8 @@
     slots = cell.shape[1]
     size = groups * local
 
+    load = pltpu.make_async_copy(ens_hbm, ens, load_sem)
+    load.start()
     barrier = pltpu.get_barrier_semaphore()
     for step in range(1, groups):
         pl.semaphore_signal(
@@ -123,6 +128,7 @@
         positions = lax.broadcasted_iota(jnp.int32, (width, slots), 0)
         selector[b] = jnp.where(positions == cell[pl.ds(b, 1), :], 1.0, 0.0).astype(BF16)
 
+    load.wait()
     pl.semaphore_wait(barrier, groups - 1)
 
     def columns(owner, b):
@@ -132,8 +138,7 @@
     def members_of(owner):
         return pl.ds(pl.multiple_of(owner * local, local), local)
 
-    @pl.loop(0, blocks)
-    def _(i):
+    def send_block(i):
         b = lax.rem(i + blocks - 1, blocks)
         for step in range(1, groups):
             peer = lax.rem(me + step, groups)
@@ -149,6 +154,14 @@
             ens.at[:, columns(me, b)], arrived.at[b, members_of(me), :], fwd_recv.at[b]
         ).start()
 
+    for i in range(min(WINDOW, blocks)):
+        send_block(i)
+
+    def send_ahead(i):
+        @pl.when(i + WINDOW < blocks)
+        def _():
+            send_block(i + WINDOW)
+
     def form_gram(slot):
         held = rows[slot]
         gram[slot] = lax.dot_general(
@@ -157,6 +170,7 @@
 
     def take_block(b):
         pltpu.make_async_copy(arrived.at[b], arrived.at[b], fwd_recv.at[b]).wait()
+        send_ahead(lax.rem(jnp.int32(b) + 1, blocks))
         alive = lax.broadcasted_iota(jnp.int32, (1, slots), 1) < count[0, b]
         root = jnp.where(alive, weight[pl.ds(b, 1), :], 0.0)
         rows[b + 1] = observed_rows(arrived[b], selector[b], value[pl.ds(b, 1), :], root)
@@ -237,8 +251,8 @@
     return pl.pallas_call(
         functools.partial(kernel, groups),
         out_shape=jax.ShapeDtypeStruct(ensemble.shape, BF16),
-        in_specs=[whole, whole, pl.BlockSpec(memory_space=pltpu.SMEM), whole, whole],
-        out_specs=whole,
+        in_specs=[pl.BlockSpec(memory_space=pl.ANY), whole, pl.BlockSpec(memory_space=pltpu.SMEM), whole, whole],
+        out_specs=pl.BlockSpec(memory_space=pl.ANY),
         scratch_shapes=[
             pltpu.VMEM((blocks, size, width), BF16),
             pltpu.VMEM((blocks + 2, size + 16, slots), BF16),
@@ -246,6 +260,8 @@
             pltpu.VMEM((blocks, width, slots), BF16),
             pltpu.VMEM((blocks, size, width), BF16),
             pltpu.VMEM((blocks, slots), F32),
+            pltpu.VMEM(ensemble.shape, BF16),
+            pltpu.SemaphoreType.DMA,
             pltpu.SemaphoreType.DMA,
             pltpu.SemaphoreType.DMA,
             pltpu.SemaphoreType.DMA((blocks,)),

time: 62.4 us -> 56.6 us (0.907)
  Pallas kernels: 59.9 us -> 54.1 us
    pallas_call x1, Pallas kernels: 59.9 us -> 54.1 us  [fused(): pl.pallas_call(functools.partial(kernel, groups), out_shape=jax.ShapeDtyp...]
where the time goes in v2:
time: 56.6 us; the launch traced here: 56.4 us
  Pallas kernels  54.1 us (96%)
  local copies, waits for them, and re-layouts  2.26 us (4%)
    pallas_call x1, Pallas kernels, fused(): pl.pallas_call(functools.partial(kernel, groups), out_shape=jax.ShapeDtyp...  54.1 us
    unnamed x1, local copies, waits for them, and re-layouts  2.26 us

profile of v2, /device:TPU:0, one launch (start us, length us, event | category | flops | bytes accessed | tf_op | source)
XLA Modules:
  0.0 56.4 jit_solution(1517722608645243533)
XLA Ops:
  0.0 54.1 %letkf.1 = bf16[16,32768]{1,0:T(8,128)(2,1)} custom-call(bf16[16,32768]{1,0:T(8,128)(2,1)} %ens_hbm.1, s32[8,256]{1,0:T(8,128)} %bitcast.3, s32[1,8]{1,0:T(1,128)} %count.1, f32[8,256]{1,0:T(8,128)} %bitcast.4, f32[8,256]{1,0:T(8,128)} %bitcast.5), custom_call_target="tpu_custom_call" | custom-call | tf_op jit(solution)/shard_map/letkf/pallas_call | solution.py:251
  54.1 2.3 %copy.7 = bf16[16,32768]{1,0:T(8,128)(2,1)} copy(bf16[16,32768]{1,0:T(8,128)(2,1)} %letkf.1) | data formatting | bytes 2097152

commit v3 on v2

--- a/solution.py
+++ b/solution.py
@@ -86,10 +86,10 @@
 def kernel(
     groups,
     ens_hbm,
-    cell,
-    count,
-    value,
-    rinv,
+    cell_hbm,
+    count_hbm,
+    value_hbm,
+    rinv_hbm,
     out,
     arrived,
     rows,
@@ -98,6 +98,10 @@
     stage,
     weight,
     ens,
+    cell,
+    count,
+    value,
+    rinv,
     load_sem,
     own_sem,
     fwd_send,
@@ -113,22 +117,27 @@
     slots = cell.shape[1]
     size = groups * local
 
-    load = pltpu.make_async_copy(ens_hbm, ens, load_sem)
-    load.start()
     barrier = pltpu.get_barrier_semaphore()
     for step in range(1, groups):
         pl.semaphore_signal(
             barrier, inc=1, device_id={"mem": lax.rem(me + step, groups)}, device_id_type=MESH
         )
 
-    weight[...] = jnp.sqrt(rinv[...])
-
-    @pl.loop(0, blocks)
-    def _(b):
-        positions = lax.broadcasted_iota(jnp.int32, (width, slots), 0)
-        selector[b] = jnp.where(positions == cell[pl.ds(b, 1), :], 1.0, 0.0).astype(BF16)
-
-    load.wait()
+    loads = [
+        pltpu.make_async_copy(source, target, load_sem.at[i])
+        for i, (source, target) in enumerate(
+            (
+                (ens_hbm, ens),
+                (cell_hbm, cell),
+                (count_hbm, count),
+                (value_hbm, value),
+                (rinv_hbm, rinv),
+            )
+        )
+    ]
+    for load in loads:
+        load.start()
+    loads[0].wait()
     pl.semaphore_wait(barrier, groups - 1)
 
     def columns(owner, b):
@@ -161,6 +170,15 @@
         @pl.when(i + WINDOW < blocks)
         def _():
             send_block(i + WINDOW)
+
+    for load in loads[1:]:
+        load.wait()
+    weight[...] = jnp.sqrt(rinv[...])
+
+    @pl.loop(0, blocks)
+    def _(b):
+        positions = lax.broadcasted_iota(jnp.int32, (width, slots), 0)
+        selector[b] = jnp.where(positions == cell[pl.ds(b, 1), :], 1.0, 0.0).astype(BF16)
 
     def form_gram(slot):
         held = rows[slot]
@@ -250,9 +268,9 @@
     whole = pl.BlockSpec(memory_space=pltpu.VMEM)
     return pl.pallas_call(
         functools.partial(kernel, groups),
-        out_shape=jax.ShapeDtypeStruct(ensemble.shape, BF16),
-        in_specs=[pl.BlockSpec(memory_space=pl.ANY), whole, pl.BlockSpec(memory_space=pltpu.SMEM), whole, whole],
-        out_specs=pl.BlockSpec(memory_space=pl.ANY),
+        out_shape=pltpu.VMEM(ensemble.shape, BF16),
+        in_specs=[pl.BlockSpec(memory_space=pl.ANY)] * 5,
+        out_specs=whole,
         scratch_shapes=[
             pltpu.VMEM((blocks, size, width), BF16),
             pltpu.VMEM((blocks + 2, size + 16, slots), BF16),
@@ -261,7 +279,11 @@
             pltpu.VMEM((blocks, size, width), BF16),
             pltpu.VMEM((blocks, slots), F32),
             pltpu.VMEM(ensemble.shape, BF16),
-            pltpu.SemaphoreType.DMA,
+            pltpu.VMEM((blocks, slots), jnp.int32),
+            pltpu.SMEM(obs_count.shape, jnp.int32),
+            pltpu.VMEM((blocks, slots), F32),
+            pltpu.VMEM((blocks, slots), F32),
+            pltpu.SemaphoreType.DMA((5,)),
             pltpu.SemaphoreType.DMA,
             pltpu.SemaphoreType.DMA,
             pltpu.SemaphoreType.DMA((blocks,)),

time: 56.6 us -> 54.3 us (0.959)
  local copies, waits for them, and re-layouts: 2.26 us -> 0.97 us
  Pallas kernels: 54.1 us -> 53.2 us
    unnamed x1, local copies, waits for them, and re-layouts: 2.26 us -> 0.97 us
    pallas_call x1, Pallas kernels: 54.1 us -> 53.2 us  [fused(): pl.pallas_call(functools.partial(kernel, groups), out_shape=pltpu.VMEM(en...]
where the time goes in v3:
time: 54.3 us; the launch traced here: 54.1 us
  Pallas kernels  53.2 us (98%)
  local copies, waits for them, and re-layouts  0.97 us (2%)
    pallas_call x1, Pallas kernels, fused(): pl.pallas_call(functools.partial(kernel, groups), out_shape=pltpu.VMEM(en...  53.2 us

profile of v3, /device:TPU:0, one launch (start us, length us, event | category | flops | bytes accessed | tf_op | source)
XLA Modules:
  0.0 54.1 jit_solution(16212374789092479191)
XLA Ops:
  0.0 53.2 %letkf.1 = bf16[16,32768]{1,0:T(8,128)(2,1)S(1)} custom-call(bf16[16,32768]{1,0:T(8,128)(2,1)} %ens_hbm.1, s32[8,256]{1,0:T(8,128)} %bitcast.3, s32[1,8]{1,0:T(1,128)} %count_hbm.1, f32[8,256]{1,0:T(8,128)} %bitcast.4, f32[8,256]{1,0:T(8,128)} %bitcast.5), custom_call_target="tpu_custom_call" | custom-call | tf_op jit(solution)/shard_map/letkf/pallas_call | solution.py:269
  53.2 1.0 %copy.7 = bf16[16,32768]{1,0:T(8,128)(2,1)} copy(bf16[16,32768]{1,0:T(8,128)(2,1)S(1)} %letkf.1) | data formatting | bytes 2097152

commit v4 on v3

--- a/solution.py
+++ b/solution.py
@@ -94,6 +94,8 @@
     arrived,
     rows,
     gram,
+    edge,
+    far_edge,
     selector,
     stage,
     weight,
@@ -210,29 +212,29 @@
             stage.at[b, members_of(me), :], out.at[:, columns(me, b)], own_sem
         ).start()
 
-    def halo(source, target, peer, which):
+    def halo(slot, peer, which):
+        edge[which] = gram[slot].astype(BF16)
         return pltpu.make_async_remote_copy(
-            src_ref=rows.at[source],
-            dst_ref=rows.at[target],
+            src_ref=edge.at[which],
+            dst_ref=far_edge.at[which],
             send_sem=halo_send.at[which],
             recv_sem=halo_recv.at[which],
             device_id={"mem": peer},
             device_id_type=MESH,
         )
 
-    upward = halo(blocks, 0, lax.rem(me + 1, groups), 0)
-    downward = halo(1, blocks + 1, lax.rem(me + groups - 1, groups), 1)
-
     take_block(blocks - 1)
+    form_gram(blocks)
+    upward = halo(blocks, lax.rem(me + 1, groups), 0)
     upward.start()
-    form_gram(blocks)
     take_block(0)
+    form_gram(1)
+    downward = halo(1, lax.rem(me + groups - 1, groups), 1)
     downward.start()
-    form_gram(1)
     take_block(1)
     form_gram(2)
     upward.wait_recv()
-    form_gram(0)
+    gram[0] = far_edge[0].astype(F32)
     give_block(0)
 
     @pl.loop(2, blocks - 1)
@@ -242,7 +244,7 @@
         give_block(b - 1)
 
     downward.wait_recv()
-    form_gram(blocks + 1)
+    gram[blocks + 1] = far_edge[1].astype(F32)
 
     @pl.loop(blocks - 2, blocks)
     def _(b):
@@ -275,6 +277,8 @@
             pltpu.VMEM((blocks, size, width), BF16),
             pltpu.VMEM((blocks + 2, size + 16, slots), BF16),
             pltpu.VMEM((blocks + 2, size + 16, size), F32),
+            pltpu.VMEM((2, size + 16, size), BF16),
+            pltpu.VMEM((2, size + 16, size), BF16),
             pltpu.VMEM((blocks, width, slots), BF16),
             pltpu.VMEM((blocks, size, width), BF16),
             pltpu.VMEM((blocks, slots), F32),

time: 54.3 us -> 53.4 us (0.983)
  Pallas kernels: 53.2 us -> 52.3 us
    pallas_call x1, Pallas kernels: 53.2 us -> 52.3 us  [fused(): pl.pallas_call(functools.partial(kernel, groups), out_shape=pltpu.VMEM(en...]
where the time goes in v4:
time: 53.4 us; the launch traced here: 53.3 us
  Pallas kernels  52.3 us (98%)
  local copies, waits for them, and re-layouts  0.97 us (2%)
    pallas_call x1, Pallas kernels, fused(): pl.pallas_call(functools.partial(kernel, groups), out_shape=pltpu.VMEM(en...  52.3 us

profile of v4, /device:TPU:0, one launch (start us, length us, event | category | flops | bytes accessed | tf_op | source)
XLA Modules:
  0.0 53.3 jit_solution(5085550031346106889)
XLA Ops:
  0.0 52.3 %letkf.1 = bf16[16,32768]{1,0:T(8,128)(2,1)S(1)} custom-call(bf16[16,32768]{1,0:T(8,128)(2,1)} %ens_hbm.1, s32[8,256]{1,0:T(8,128)} %bitcast.3, s32[1,8]{1,0:T(1,128)} %count_hbm.1, f32[8,256]{1,0:T(8,128)} %bitcast.4, f32[8,256]{1,0:T(8,128)} %bitcast.5), custom_call_target="tpu_custom_call" | custom-call | tf_op jit(solution)/shard_map/letkf/pallas_call | solution.py:271
  52.3 1.0 %copy.7 = bf16[16,32768]{1,0:T(8,128)(2,1)} copy(bf16[16,32768]{1,0:T(8,128)(2,1)S(1)} %letkf.1) | data formatting | bytes 2097152

commit v5 on v4

--- a/solution.py
+++ b/solution.py
@@ -197,20 +197,26 @@
 
     def give_block(b):
         localized = gram[b + 1] + localize * (gram[b] + gram[b + 2])
-        stage[b] = increments_of(localized, arrived[b])
-        for step in range(1, groups):
-            peer = lax.rem(me + step, groups)
-            pltpu.make_async_remote_copy(
-                src_ref=stage.at[b, members_of(peer), :],
-                dst_ref=out.at[:, columns(me, b)],
-                send_sem=ret_send,
-                recv_sem=ret_recv,
-                device_id={"mem": peer},
-                device_id_type=MESH,
+        pair = b // 2
+        part = pl.ds(pl.multiple_of((b % 2) * width, width), width)
+        stage[pair, :, part] = increments_of(localized, arrived[b])
+
+        @pl.when(b % 2 == 1)
+        def _():
+            both = pl.ds(pl.multiple_of((me * blocks + b - 1) * width, width), 2 * width)
+            for step in range(1, groups):
+                peer = lax.rem(me + step, groups)
+                pltpu.make_async_remote_copy(
+                    src_ref=stage.at[pair, members_of(peer), :],
+                    dst_ref=out.at[:, both],
+                    send_sem=ret_send,
+                    recv_sem=ret_recv,
+                    device_id={"mem": peer},
+                    device_id_type=MESH,
+                ).start()
+            pltpu.make_async_copy(
+                stage.at[pair, members_of(me), :], out.at[:, both], own_sem
             ).start()
-        pltpu.make_async_copy(
-            stage.at[b, members_of(me), :], out.at[:, columns(me, b)], own_sem
-        ).start()
 
     def halo(slot, peer, which):
         edge[which] = gram[slot].astype(BF16)
@@ -235,7 +241,7 @@
     form_gram(2)
     upward.wait_recv()
     gram[0] = far_edge[0].astype(F32)
-    give_block(0)
+    give_block(jnp.int32(0))
 
     @pl.loop(2, blocks - 1)
     def _(b):
@@ -280,7 +286,7 @@
             pltpu.VMEM((2, size + 16, size), BF16),
             pltpu.VMEM((2, size + 16, size), BF16),
             pltpu.VMEM((blocks, width, slots), BF16),
-            pltpu.VMEM((blocks, size, width), BF16),
+            pltpu.VMEM((blocks // 2, size, 2 * width), BF16),
             pltpu.VMEM((blocks, slots), F32),
             pltpu.VMEM(ensemble.shape, BF16),
             pltpu.VMEM((blocks, slots), jnp.int32),
@@ -392,7 +398,7 @@
     blocks, slots = observations[0].shape[1:]
     width = cells // (groups * blocks)
     aligned = local % 16 == 0 and width % 128 == 0 and slots % 128 == 0
-    aligned = aligned and (groups * local) % 128 == 0 and groups > 1 and blocks > 2
+    aligned = aligned and (groups * local) % 128 == 0 and groups > 1 and blocks > 2 and blocks % 2 == 0
     return (fused if aligned else on_device)(ensemble, *observations)
 
 

time: 53.4 us -> 52.8 us (0.989)
  Pallas kernels: 52.3 us -> 51.7 us
    pallas_call x1, Pallas kernels: 52.3 us -> 51.7 us  [fused(): pl.pallas_call(functools.partial(kernel, groups), out_shape=pltpu.VMEM(en...]
where the time goes in v5:
time: 52.8 us; the launch traced here: 52.7 us
  Pallas kernels  51.7 us (98%)
  local copies, waits for them, and re-layouts  0.97 us (2%)
    pallas_call x1, Pallas kernels, fused(): pl.pallas_call(functools.partial(kernel, groups), out_shape=pltpu.VMEM(en...  51.7 us

profile of v5, /device:TPU:0, one launch (start us, length us, event | category | flops | bytes accessed | tf_op | source)
XLA Modules:
  0.0 52.7 jit_solution(2781497119645629781)
XLA Ops:
  0.0 51.7 %letkf.1 = bf16[16,32768]{1,0:T(8,128)(2,1)S(1)} custom-call(bf16[16,32768]{1,0:T(8,128)(2,1)} %ens_hbm.1, s32[8,256]{1,0:T(8,128)} %bitcast.3, s32[1,8]{1,0:T(1,128)} %count_hbm.1, f32[8,256]{1,0:T(8,128)} %bitcast.4, f32[8,256]{1,0:T(8,128)} %bitcast.5), custom_call_target="tpu_custom_call" | custom-call | tf_op jit(solution)/shard_map/letkf/pallas_call | solution.py:277
  51.7 1.0 %copy.7 = bf16[16,32768]{1,0:T(8,128)(2,1)} copy(bf16[16,32768]{1,0:T(8,128)(2,1)S(1)} %letkf.1) | data formatting | bytes 2097152
